TPU v7x, 32 devices: a whole 2x2x4 slice. The times are simulated.
32 devices in a mesh: grp: 4 (over y, x), slab: 8 (over z, core).
Axes of the slice: x: 2, y: 2, z: 4, core: 2. Of those that a mesh axis runs over, the one named last changes fastest.
Arguments:
- state: float32 [4, 2, 256, 128, 256], P(None, None, 'grp', 'slab'), may hold values from -5.6 to 5.6
- kz_group: int32 [256], replicated, may hold values from 0 to 7, as said below
- cutoffs: int32 [3], replicated, may hold values from 28 to 32
- damping: float32 [8], replicated, may hold values from 0.005 to 0.5
- power: float32 [8], replicated, may hold values from 0.2 to 4
Outputs:
- new_state: float32 [4, 2, 256, 128, 256], P(None, None, 'grp', 'slab')
Inputs may be any that keep to these rules, and one draw needn't show every extreme that they name: `kz_group`: each of the 8 groups holds exactly 32 indices.
All inputs are finite; a program needn't handle non-finite values.
Results may differ from a plain program's by a relative error of at most 0.00005.
Values sent between devices are 32-bit elements; how exact they have to be, the bound alone decides.
A program may use at most 192 MiB of HBM per device.

v0:
```python
import math
import jax
import jax.numpy as jnp
from jax import lax
from jax.sharding import PartitionSpec as P

NX = 256
NY = 256
NZ = 256
GROUPS = 8
KX = 128
GMODES = 32
PRECISE = lax.Precision.HIGHEST
TWO_PI = 6.283185307179586
TIME_STEP = 0.25
CORIOLIS = 1.0
BRUNT_SQUARED = 2.0
EPSILON = 1e-06


def signed(index, length):
    return jnp.where(index < length // 2, index, index - length)


def angles(modes, points, length):
    phase = modes[:, None] * points[None, :] % length
    theta = phase.astype(jnp.float32) * (TWO_PI / length)
    return (jnp.cos(theta), jnp.sin(theta))


def rotate(pattern, real_part, imag_part, cosine_table, sine_table, forward):
    first = jnp.einsum(pattern, real_part, cosine_table, precision=PRECISE)
    second = jnp.einsum(pattern, imag_part, sine_table, precision=PRECISE)
    third = jnp.einsum(pattern, real_part, sine_table, precision=PRECISE)
    fourth = jnp.einsum(pattern, imag_part, cosine_table, precision=PRECISE)
    if forward:
        return (first + second, fourth - third)
    return (first - second, third + fourth)


def times_i(entries):
    return jnp.stack([-entries[1], entries[0]])


def x_forward(products, pattern, cosine_table, sine_table):
    real_x = jnp.einsum(pattern, products, cosine_table, precision=PRECISE)
    imag_x = -jnp.einsum(pattern, products, sine_table, precision=PRECISE)
    return (real_x, imag_x)


def shards(state, kz_group, cutoffs, damping, power):
    grp_count = lax.axis_size("grp")
    grp_index = lax.axis_index("grp")
    slab_index = lax.axis_index("slab")
    slots_here = state.shape[2]
    cols_here = state.shape[3]
    groups_here = GROUPS // grp_count
    normalizer = 1.0 / math.sqrt(NX * NY * NZ)
    slot_mode = jnp.argsort(kz_group, stable=True)
    local_mode = lax.dynamic_slice_in_dim(slot_mode, grp_index * slots_here, slots_here)
    mode_z = signed(local_mode, NZ)
    mode_x = slab_index * cols_here + jnp.arange(cols_here, dtype=jnp.int32)
    mode_y = signed(jnp.arange(NY, dtype=jnp.int32), NY)
    wave_z = (TWO_PI / NZ * mode_z.astype(jnp.float32))[:, None, None]
    wave_x = (TWO_PI / NX * mode_x.astype(jnp.float32))[None, :, None]
    wave_y = (TWO_PI / NY * mode_y.astype(jnp.float32))[None, None, :]
    flow_x, flow_y, flow_z, buoyant = (state[0], state[1], state[2], state[3])
    means = None
    swirl_x = times_i(wave_y * flow_z - wave_z * flow_y)
    swirl_y = times_i(wave_z * flow_x - wave_x * flow_z)
    swirl_z = times_i(wave_x * flow_y - wave_y * flow_x)
    fields = jnp.stack([flow_x, flow_y, flow_z, buoyant, swirl_x, swirl_y, swirl_z])
    cosine_y, sine_y = angles(jnp.arange(NY, dtype=jnp.int32), jnp.arange(NY, dtype=jnp.int32), NY)
    real_y, imag_y = rotate("fzxm,my->fzxy", fields[:, 0], fields[:, 1], cosine_y, sine_y, False)
    spectral_y = jnp.stack([real_y, imag_y], axis=1)
    cosine_zi, sine_zi = angles(slot_mode, jnp.arange(NZ, dtype=jnp.int32), NZ)
    cosine_zf, sine_zf = angles(jnp.arange(NZ, dtype=jnp.int32), slot_mode, NZ)
    weights = jnp.where(jnp.arange(KX) == 0, 1.0, 2.0).astype(jnp.float32) * normalizer
    cosine_x, sine_x = angles(jnp.arange(KX, dtype=jnp.int32), jnp.arange(NX, dtype=jnp.int32), NX)
    cosine_x = cosine_x * weights[:, None]
    sine_x = sine_x * weights[:, None]
    cosine_xf, sine_xf = angles(
        jnp.arange(NX, dtype=jnp.int32), jnp.arange(KX, dtype=jnp.int32), NX
    )
    pieces = lax.all_to_all(spectral_y, "grp", split_axis=4, concat_axis=2, tiled=True)
    real_part, imag_part = rotate(
        "fsxy,sz->fzxy", pieces[:, 0], pieces[:, 1], cosine_zi, sine_zi, False
    )
    grid_z = jnp.stack([real_part, imag_part], axis=1)
    pieces = lax.all_to_all(grid_z, "slab", split_axis=2, concat_axis=3, tiled=True)
    physical = jnp.einsum("fzky,kn->fzyn", pieces[:, 0], cosine_x, precision=PRECISE) - jnp.einsum(
        "fzky,kn->fzyn", pieces[:, 1], sine_x, precision=PRECISE
    )
    grid_u = physical[0]
    grid_v = physical[1]
    grid_w = physical[2]
    grid_b = physical[3]
    grid_ox = physical[4]
    grid_oy = physical[5]
    grid_oz = physical[6]
    products = jnp.stack(
        [
            grid_v * grid_oz - grid_w * grid_oy,
            grid_w * grid_ox - grid_u * grid_oz,
            grid_u * grid_oy - grid_v * grid_ox,
            grid_u * grid_b,
            grid_v * grid_b,
            grid_w * grid_b,
        ]
    )
    real_x, imag_x = x_forward(products, "fzyn,nk->fzky", cosine_xf, sine_xf)
    sectioned = jnp.stack([real_x, imag_x], axis=1)
    pieces = lax.all_to_all(sectioned, "slab", split_axis=3, concat_axis=2, tiled=True)
    real_part, imag_part = rotate(
        "fzxy,zs->fsxy", pieces[:, 0], pieces[:, 1], cosine_zf, sine_zf, True
    )
    spectral_z = jnp.stack([real_part, imag_part], axis=1)
    pieces = lax.all_to_all(spectral_z, "grp", split_axis=2, concat_axis=4, tiled=True)
    real_part, imag_part = rotate(
        "fsxy,ym->fsxm", pieces[:, 0], pieces[:, 1], cosine_y, sine_y, True
    )
    tendency = jnp.stack([real_part, imag_part], axis=1) * normalizer
    real_part = state[:, 0]
    imag_part = state[:, 1]
    cell_flux = real_part[2] * real_part[3] + imag_part[2] * imag_part[3]
    cell_energy = 0.5 * (
        jnp.sum(real_part[:3] ** 2 + imag_part[:3] ** 2, axis=0)
        + (real_part[3] ** 2 + imag_part[3] ** 2) / BRUNT_SQUARED
    )
    partial_value = jnp.stack(
        [jnp.sum(cell_flux, axis=(1, 2)), jnp.sum(cell_energy, axis=(1, 2))], axis=1
    )
    partial_value = jnp.sum(partial_value.reshape(groups_here, GMODES, 2), axis=1)
    totals = lax.psum(partial_value, "slab")
    means = totals / (GMODES * KX * NY)
    kept = (
        (96 * jnp.abs(mode_z) <= cutoffs[2] * NZ)[:, None, None]
        & (96 * mode_x <= cutoffs[0] * NX)[None, :, None]
        & (96 * jnp.abs(mode_y) <= cutoffs[1] * NY)[None, None, :]
    ).astype(jnp.float32)
    moment_x, moment_y, moment_z = (tendency[0] * kept, tendency[1] * kept, tendency[2] * kept)
    divergence = wave_x * tendency[3] + wave_y * tendency[4] + wave_z * tendency[5]
    source_b = jnp.stack([divergence[1], -divergence[0]]) * kept
    power_here = lax.dynamic_slice_in_dim(power, grp_index * groups_here, groups_here)
    damping_here = lax.dynamic_slice_in_dim(damping, grp_index * groups_here, groups_here)
    forcing = (power_here - means[:, 0]) / (2.0 * (means[:, 1] + EPSILON))
    forcing_slot = jnp.repeat(forcing, GMODES)[:, None, None]
    damping_slot = jnp.repeat(damping_here, GMODES)[:, None, None]
    right_x = flow_x + TIME_STEP * (moment_x + forcing_slot * flow_x)
    right_y = flow_y + TIME_STEP * (moment_y + forcing_slot * flow_y)
    right_z = flow_z + TIME_STEP * (moment_z + forcing_slot * flow_z)
    right_b = buoyant + TIME_STEP * source_b
    wave_sq = wave_x * wave_x + wave_y * wave_y + wave_z * wave_z
    implicit = 1.0 + TIME_STEP * damping_slot * wave_sq
    rotation = TIME_STEP * CORIOLIS
    first_den = implicit * implicit + rotation * rotation
    second_den = implicit * implicit + TIME_STEP * TIME_STEP * BRUNT_SQUARED
    new_x = (implicit * right_x + rotation * right_y) / first_den
    new_y = (implicit * right_y - rotation * right_x) / first_den
    new_z = (implicit * right_z + TIME_STEP * right_b) / second_den
    new_b = (implicit * right_b - TIME_STEP * BRUNT_SQUARED * right_z) / second_den
    inverse_sq = 1.0 / (wave_sq + (wave_sq == 0).astype(jnp.float32))
    inner = (wave_x * new_x + wave_y * new_y + wave_z * new_z) * inverse_sq
    new_x = new_x - wave_x * inner
    new_y = new_y - wave_y * inner
    new_z = new_z - wave_z * inner
    return jnp.stack([new_x, new_y, new_z, new_b])


def solution(mesh):
    return jax.shard_map(
        shards,
        mesh=mesh,
        in_specs=(P(None, None, "grp", "slab", None), P(), P(), P(), P()),
        out_specs=P(None, None, "grp", "slab", None),
        check_vma=False,
    )
```

profile of v0, /device:TPU:0, one launch (start us, length us, event | category | flops | bytes accessed | tf_op | source)
XLA Modules:
  0.0 2021.2 jit_solution(9663195333022750134)
XLA Ops:
  30.6 10.1 subtract_bitcast_fusion.1
  40.7 10.2 add_bitcast_fusion.1
  50.9 12.4 pad_maximum_fusion.1
  63.3 27.2 %copy.46 = f32[7,2,64,16,256]{2,3,1,0,4:T(8,128)} copy(f32[7,2,64,16,256]{4,3,2,0,1:T(8,128)} %pad_maximum_fusion.1) | data formatting | bytes 29360128 | tf_op jit(solution)/shard_map/stack | solution.py:75
  90.5 37.7 %reshape.239 = f32[4,1,917504]{2,1,0:T(1,128)} reshape(f32[256,7,2,16,64]{4,3,2,1,0:T(8,128)} %bitcast.261) | data formatting | bytes 29360128
  128.2 172.1 %all_to_all.72 = f32[4,1,917504]{2,1,0:T(1,128)} all-to-all(f32[4,1,917504]{2,1,0:T(1,128)} %reshape.239), channel_id=1, replica_groups=mesh['grp'=4,'slab'=8] {'grp'}, dimensions={0} | all-to-all | bytes 29360128 | tf_op jit(solution)/shard_map/all_to_all | solution.py:85
  300.8 46.1 %reduce.2 = f32[4,917504]{1,0:T(4,128)} reduce(f32[4,1,917504]{2,1,0:T(1,128)} %all_to_all.72, f32[]{:T(128)} %broadcast.529), dimensions={1}, to_apply=%all_to_all.52.reduce_sub_computation | reduce | bytes 29360132 | tf_op jit(solution)/shard_map/all_to_all | solution.py:85
  346.9 42.0 %reshape.240 = f32[256,7,2,16,64]{4,3,2,1,0:T(8,128)} reshape(f32[4,917504]{1,0:T(4,128)} %reduce.2) | data formatting | bytes 29360128
  388.9 33.7 %copy.76 = f32[7,2,64,16,4,64]{2,4,5,3,0,1:T(4,128)} copy(f32[7,2,64,16,4,64]{2,3,1,0,5,4:T(8,128)} %bitcast.258) | data formatting | bytes 29360128 | tf_op jit(solution)/shard_map/all_to_all | solution.py:85
  422.6 26.9 %all_to_all.55 = f32[7,2,256,16,64]{2,4,3,0,1:T(8,128)} reshape(f32[7,2,4,64,16,64]{3,2,5,4,0,1:T(4,128)} %bitcast.259) | data formatting | bytes 29360128 | tf_op jit(solution)/shard_map/all_to_all | solution.py:85
  449.5 13.3 fusion.204
  462.8 12.8 fusion.99
  482.6 10.2 fusion.95
  492.8 10.4 fusion.97
  503.2 10.5 subtract_bitcast_fusion
  522.1 13.1 pad_maximum_fusion.2
  535.2 27.2 %copy.48 = f32[7,2,256,16,64]{4,3,0,1,2:T(8,128)} copy(f32[7,2,256,16,64]{2,4,3,0,1:T(8,128)} %pad_maximum_fusion.2) | data formatting | bytes 29360128 | tf_op jit(solution)/shard_map/stack | solution.py:89
  562.4 23.1 %reshape.241 = f32[8,1,458752]{2,1,0:T(1,128)} reshape(f32[256,2,7,16,64]{4,3,2,1,0:T(8,128)} %bitcast.262) | data formatting | bytes 29360128
  591.1 318.7 %all-to-all-done.1 = f32[8,1,458752]{2,1,0:T(1,128)} async-done(((f32[8,1,458752]{2,1,0:T(1,128)}), f32[8,1,458752]{2,1,0:T(1,128)}, u32[]{:S(2)}, u32[]{:S(2)}) %all-to-all-start.1) | async-done | bytes 14680096 | tf_op jit(solution)/shard_map/all_to_all | solution.py:90
  909.7 42.5 %reduce.3 = f32[8,458752]{1,0:T(8,128)} reduce(f32[8,1,458752]{2,1,0:T(1,128)} %all-to-all-done.1, f32[]{:T(128)} %broadcast.529), dimensions={1}, to_apply=%all_to_all.56.reduce_sub_computation | reduce | bytes 29360132 | tf_op jit(solution)/shard_map/all_to_all | solution.py:90
  952.2 26.2 %reshape.242 = f32[256,2,7,16,64]{4,3,2,1,0:T(8,128)} reshape(f32[8,458752]{1,0:T(8,128)} %reduce.3) | data formatting | bytes 29360128
  978.5 22.4 %copy.50 = f32[7,2,32,8,16,64]{5,4,3,2,1,0:T(8,128)} copy(f32[7,2,32,8,16,64]{5,4,0,1,2,3:T(8,128)} %bitcast.260) | data formatting | bytes 29360128 | tf_op jit(solution)/shard_map/all_to_all | solution.py:90
  1000.9 30.6 %fusion = f32[7,32,64,256]{3,2,1,0:T(8,128)} fusion(f32[7,2,32,128,64]{4,3,2,1,0:T(8,128)} %bitcast.256, f32[128]{0:T(128)S(1)} %fusion.119), kind=kOutput, calls=%fused_computation.3 | convolution fusion | flops 5637636096 | bytes 29360640 | tf_op jit(solution)/shard_map/fzky,kn->fzyn/dot_general | solution.py:91
  1031.5 32.3 %fusion.2 = f32[7,32,64,256]{3,2,1,0:T(8,128)} fusion(f32[7,32,64,256]{3,2,1,0:T(8,128)} %fusion, f32[7,2,32,128,64]{4,3,2,1,0:T(8,128)} %bitcast.257, f32[128]{0:T(128)S(1)} %fusion.119), kind=kOutput, calls=%fused_computation.12 | convolution fusion | flops 5641306112 | bytes 44040704 | tf_op jit(solution)/shard_map/fzky,kn->fzyn/dot_general | solution.py:91
  1076.0 11.5 convolution_bitcast_fusion
  1087.5 12.8 negate_bitcast_fusion
  1100.3 9.4 pad_maximum_fusion.3
  1109.7 23.4 %copy.53 = f32[6,2,32,128,64]{4,2,0,1,3:T(8,128)} copy(f32[6,2,32,128,64]{3,4,2,0,1:T(8,128)} %pad_maximum_fusion.3) | data formatting | bytes 25165824 | tf_op jit(solution)/shard_map/stack | solution.py:112
  1133.1 20.7 %reshape.243 = f32[8,1,393216]{2,1,0:T(1,128)} reshape(f32[128,2,6,32,64]{4,3,2,1,0:T(8,128)} %bitcast.264) | data formatting | bytes 25165824
  1153.8 280.5 %all_to_all.73 = f32[8,1,393216]{2,1,0:T(1,128)} all-to-all(f32[8,1,393216]{2,1,0:T(1,128)} %reshape.243), channel_id=1, replica_groups=mesh['grp'=4,'slab'=8] {'slab'}, dimensions={0} | all-to-all | bytes 25165824 | tf_op jit(solution)/shard_map/all_to_all | solution.py:113
  1434.2 36.7 %reduce.4 = f32[8,393216]{1,0:T(8,128)} reduce(f32[8,1,393216]{2,1,0:T(1,128)} %all_to_all.73, f32[]{:T(128)} %broadcast.529), dimensions={1}, to_apply=%all_to_all.60.reduce_sub_computation | reduce | bytes 25165828 | tf_op jit(solution)/shard_map/all_to_all | solution.py:113
  1470.9 22.6 %reshape.244 = f32[128,2,6,32,64]{4,3,2,1,0:T(8,128)} reshape(f32[8,393216]{1,0:T(8,128)} %reduce.4) | data formatting | bytes 25165824
  1493.5 28.3 %copy.55 = f32[6,2,8,32,16,64]{5,4,3,2,1,0:T(8,128)} copy(f32[6,2,8,32,16,64]{5,3,0,1,4,2:T(8,128)} %bitcast.265) | data formatting | bytes 25165824 | tf_op jit(solution)/shard_map/all_to_all | solution.py:113
  1521.8 18.0 fusion.203
  1539.8 10.8 copy.70
  1550.6 11.3 fusion.105
  1571.3 10.8 copy.71
  1582.1 11.5 fusion.109
  1610.8 11.4 pad_maximum_fusion.4
  1622.2 23.4 %copy.58 = f32[6,2,256,16,64]{4,3,0,1,2:T(8,128)} copy(f32[6,2,256,16,64]{2,4,3,0,1:T(8,128)} %pad_maximum_fusion.4) | data formatting | bytes 25165824 | tf_op jit(solution)/shard_map/stack | solution.py:117
  1645.6 33.5 %reshape.245 = f32[4,1,786432]{2,1,0:T(1,128)} reshape(f32[256,2,6,16,64]{4,3,2,1,0:T(8,128)} %bitcast.266) | data formatting | bytes 25165824
  1694.4 14.5 psum.7
  1715.6 107.0 %all-to-all-done.3 = f32[4,1,786432]{2,1,0:T(1,128)} async-done(((f32[4,1,786432]{2,1,0:T(1,128)}), f32[4,1,786432]{2,1,0:T(1,128)}, u32[]{:S(2)}, u32[]{:S(2)}) %all-to-all-start.3) | async-done | bytes 12582944 | tf_op jit(solution)/shard_map/all_to_all | solution.py:118
  1822.6 40.1 %reduce.5 = f32[4,786432]{1,0:T(4,128)} reduce(f32[4,1,786432]{2,1,0:T(1,128)} %all-to-all-done.3, f32[]{:T(128)} %broadcast.529), dimensions={1}, to_apply=%all_to_all.64.reduce_sub_computation | reduce | bytes 25165828 | tf_op jit(solution)/shard_map/all_to_all | solution.py:118
  1862.7 31.9 %reshape.246 = f32[256,2,6,16,64]{4,3,2,1,0:T(8,128)} reshape(f32[4,786432]{1,0:T(4,128)} %reduce.5) | data formatting | bytes 25165824
  1894.6 30.2 %copy.77 = f32[6,2,4,64,16,64]{5,2,4,3,0,1:T(4,128)} copy(f32[6,2,4,64,16,64]{5,4,0,1,3,2:T(8,128)} %bitcast.267) | data formatting | bytes 25165824 | tf_op jit(solution)/shard_map/all_to_all | solution.py:118
  1924.9 23.2 %all_to_all.67 = f32[6,2,64,16,256]{4,3,2,0,1:T(8,128)} reshape(f32[6,2,64,16,4,64]{5,4,3,2,0,1:T(4,128)} %bitcast.268) | data formatting | bytes 25165824 | tf_op jit(solution)/shard_map/all_to_all | solution.py:118
  1948.1 9.6 fusion.8
  (141 shorter events, 173.5 us)
Async XLA Ops:
  0.0 9.1 copy-start.17
  0.5 8.6 copy-start.22
  4.4 488.4 %copy-start.15 = (s32[256]{0:T(256)}, s32[256]{0:T(256)S(1)}, u32[]{:S(2)}) copy-start(s32[256]{0:T(256)S(1)} %get-tuple-element.6) | copy-start | bytes 3076
  5.0 4.2 copy-start.19
  9.7 2.2 slice-start
  10.1 3.2 slice-start.1
  462.8 12.9 copy-start.2
  462.8 19.8 slice-start.7
  475.7 6.9 slice-start.8
  585.5 324.3 %all-to-all-start.1 = ((f32[8,1,458752]{2,1,0:T(1,128)}), f32[8,1,458752]{2,1,0:T(1,128)}, u32[]{:S(2)}, u32[]{:S(2)}) async-start(f32[8,1,458752]{2,1,0:T(1,128)} %reshape.241), calls=%async_computation.1 | async-start | bytes 29360128 | tf_op jit(solution)/shard_map/all_to_all | solution.py:90
  1063.8 10.1 copy-start
  1539.8 10.8 copy-start.16
  1550.6 11.3 copy-start.4
  1582.1 11.5 copy-start.3
  1593.5 6.2 copy-start.6
  1599.8 6.9 copy-start.5
  1679.1 143.5 %all-to-all-start.3 = ((f32[4,1,786432]{2,1,0:T(1,128)}), f32[4,1,786432]{2,1,0:T(1,128)}, u32[]{:S(2)}, u32[]{:S(2)}) async-start(f32[4,1,786432]{2,1,0:T(1,128)} %reshape.245), calls=%async_computation.3 | async-start | bytes 25165824 | tf_op jit(solution)/shard_map/all_to_all | solution.py:118
  1685.4 23.5 %copy-start.24 = (f32[8]{0:T(128)S(1)}, f32[8]{0:T(128)}, u32[]{:S(2)}) copy-start(f32[8]{0:T(128)} %param.9) | copy-start | bytes 100
  1685.5 23.5 %copy-start.25 = (f32[8]{0:T(128)S(1)}, f32[8]{0:T(128)}, u32[]{:S(2)}) copy-start(f32[8]{0:T(128)} %param.8) | copy-start | bytes 100
  1685.5 23.7 %copy-start.21 = (s32[3]{0:T(128)S(1)}, s32[3]{0:T(128)}, u32[]{:S(2)}) copy-start(s32[3]{0:T(128)} %param.7) | copy-start | bytes 40
  1685.5 26.4 %copy-start.27 = (s32[64]{0:T(128)S(1)}, s32[64]{0:T(128)}, u32[]{:S(2)}) copy-start(s32[64]{0:T(128)} %get-tuple-element.12) | copy-start | bytes 772
  1685.5 26.5 %copy-start.26 = (f32[16]{0:T(128)S(1)}, f32[16]{0:T(128)}, u32[]{:S(2)}) copy-start(f32[16]{0:T(128)} %get-tuple-element.40) | copy-start | bytes 196
  1948.1 9.6 copy-start.1
  1979.6 8.9 copy-start.18
  1979.6 8.9 copy-start.20
  1979.6 8.9 copy-start.23
  1988.5 3.9 copy-start.7
  1988.5 3.9 copy-start.8
  1988.5 3.9 copy-start.9
  1988.5 4.0 copy-start.10
  1988.5 13.3 slice-start.2
  1992.1 9.8 slice-start.4
  1992.3 9.5 copy-start.11
  1992.3 9.5 copy-start.12
  1992.5 10.2 slice-start.3
  1992.5 11.4 slice-start.5
  1992.5 12.6 slice-start.6
  2012.8 3.5 copy-start.13
  2012.8 4.1 copy-start.14
where the time goes:
time: 2030 us; the launch traced here: 2020 us
  local copies, waits for them, and re-layouts  566 us (28%)
  blocking collectives  467 us (23%)
  waiting for transfers between devices  426 us (21%)
  other arithmetic  315 us (16%)
  matrix products  233 us (11%)
    all_to_all x1, waiting for transfers between devices, shards(): lax.all_to_all(grid_z, 'slab', split_axis=2, concat_axis=3, tiled=True)  319 us
    all_to_all x1, blocking collectives, shards(): lax.all_to_all(sectioned, 'slab', split_axis=3, concat_axis=2, tiled=True)  280 us
    unnamed x84, local copies, waits for them, and re-layouts  267 us
    all_to_all x1, blocking collectives, shards(): lax.all_to_all(spectral_y, 'grp', split_axis=4, concat_axis=2, tiled=True)  172 us
    all_to_all x1, waiting for transfers between devices, shards(): lax.all_to_all(spectral_z, 'grp', split_axis=2, concat_axis=4, tiled=True)  107 us
    unnamed x8, matrix products  78.6 us
    all_to_all x3, local copies, waits for them, and re-layouts, shards(): lax.all_to_all(spectral_y, 'grp', split_axis=4, concat_axis=2, tiled=True)  61.2 us
    all_to_all x2, local copies, waits for them, and re-layouts, shards(): lax.all_to_all(spectral_z, 'grp', split_axis=2, concat_axis=4, tiled=True)  53.4 us
  transfers between devices with their start and end apart: 2, of which 2 were waited for; matrix products, arithmetic and copies ran while one was open for 1% of the time, Pallas kernels for 0%

commit v1 on v0

--- a/solution.py
+++ b/solution.py
@@ -110,7 +110,12 @@
     )
     real_x, imag_x = x_forward(products, "fzyn,nk->fzky", cosine_xf, sine_xf)
     sectioned = jnp.stack([real_x, imag_x], axis=1)
-    pieces = lax.all_to_all(sectioned, "slab", split_axis=3, concat_axis=2, tiled=True)
+    pieces = jnp.concatenate(
+        lax.all_to_all(
+            jnp.stack(jnp.split(sectioned, lax.axis_size("slab"), axis=3)), "slab", 0, 0
+        ),
+        axis=2,
+    )
     real_part, imag_part = rotate(
         "fzxy,zs->fsxy", pieces[:, 0], pieces[:, 1], cosine_zf, sine_zf, True
     )

time: 2030 us -> 2130 us (1.049)
  local copies, waits for them, and re-layouts: 566 us -> 619 us
  other arithmetic: 315 us -> 361 us
    another operation x1 -> x9, local copies, waits for them, and re-layouts: 23.4 us -> 71.7 us  [shards(): jnp.stack(jnp.split(sectioned, lax.axis_size('slab'), axis=3))]
    another operation x1, other arithmetic: 9.43 us -> 55.2 us  [shards(): jnp.stack(jnp.split(sectioned, lax.axis_size('slab'), axis=3))]
    all_to_all x1 -> x0, local copies, waits for them, and re-layouts: 28.3 us -> none  [shards(): lax.all_to_all(sectioned, 'slab', split_axis=3, concat_axis=2, tiled=True)]
    unnamed x84 -> x103, local copies, waits for them, and re-layouts: 267 us -> 283 us
where the time goes in v1:
time: 2130 us; the launch traced here: 2120 us
  local copies, waits for them, and re-layouts  619 us (29%)
  blocking collectives  467 us (22%)
  waiting for transfers between devices  426 us (20%)
  other arithmetic  361 us (17%)
  matrix products  235 us (11%)
    all_to_all x1, waiting for transfers between devices, shards(): lax.all_to_all(grid_z, 'slab', split_axis=2, concat_axis=3, tiled=True)  319 us
    unnamed x103, local copies, waits for them, and re-layouts  283 us
    all_to_all x1, blocking collectives, shards(): lax.all_to_all(jnp.stack(jnp.split(sectioned, lax.axis_size('slab'), axis...  280 us
    all_to_all x1, blocking collectives, shards(): lax.all_to_all(spectral_y, 'grp', split_axis=4, concat_axis=2, tiled=True)  172 us
    all_to_all x1, waiting for transfers between devices, shards(): lax.all_to_all(spectral_z, 'grp', split_axis=2, concat_axis=4, tiled=True)  107 us
    unnamed x8, matrix products  81.2 us
    another operation x9, local copies, waits for them, and re-layouts, shards(): jnp.stack(jnp.split(sectioned, lax.axis_size('slab'), axis=3))  71.7 us
    all_to_all x3, local copies, waits for them, and re-layouts, shards(): lax.all_to_all(spectral_y, 'grp', split_axis=4, concat_axis=2, tiled=True)  61.1 us
  transfers between devices with their start and end apart: 2, of which 2 were waited for; matrix products, arithmetic and copies ran while one was open for 1% of the time, Pallas kernels for 0%

profile of v1, /device:TPU:0, one launch (start us, length us, event | category | flops | bytes accessed | tf_op | source)
XLA Modules:
  0.0 2123.4 jit_solution(8792782294816858971)
XLA Ops:
  30.6 10.1 add_bitcast_fusion.1
  40.7 10.3 subtract_bitcast_fusion.1
  50.9 12.4 pad_maximum_fusion.1
  63.3 27.2 %copy.50 = f32[7,2,64,16,256]{2,3,1,0,4:T(8,128)} copy(f32[7,2,64,16,256]{4,3,2,0,1:T(8,128)} %pad_maximum_fusion.1) | data formatting | bytes 29360128 | tf_op jit(solution)/shard_map/stack | solution.py:75
  90.5 37.7 %reshape.247 = f32[4,1,917504]{2,1,0:T(1,128)} reshape(f32[256,7,2,16,64]{4,3,2,1,0:T(8,128)} %bitcast.273) | data formatting | bytes 29360128
  128.2 172.0 %all_to_all.59 = f32[4,1,917504]{2,1,0:T(1,128)} all-to-all(f32[4,1,917504]{2,1,0:T(1,128)} %reshape.247), channel_id=1, replica_groups=mesh['grp'=4,'slab'=8] {'grp'}, dimensions={0} | all-to-all | bytes 29360128 | tf_op jit(solution)/shard_map/all_to_all | solution.py:85
  300.8 46.2 %reduce.2 = f32[4,917504]{1,0:T(4,128)} reduce(f32[4,1,917504]{2,1,0:T(1,128)} %all_to_all.59, f32[]{:T(128)} %broadcast.529), dimensions={1}, to_apply=%all_to_all.42.reduce_sub_computation | reduce | bytes 29360132 | tf_op jit(solution)/shard_map/all_to_all | solution.py:85
  347.0 41.8 %reshape.248 = f32[256,7,2,16,64]{4,3,2,1,0:T(8,128)} reshape(f32[4,917504]{1,0:T(4,128)} %reduce.2) | data formatting | bytes 29360128
  388.8 33.7 %copy.85 = f32[7,2,64,16,4,64]{2,4,5,3,0,1:T(4,128)} copy(f32[7,2,64,16,4,64]{2,3,1,0,5,4:T(8,128)} %bitcast.270) | data formatting | bytes 29360128 | tf_op jit(solution)/shard_map/all_to_all | solution.py:85
  422.4 26.9 %all_to_all.45 = f32[7,2,256,16,64]{2,4,3,0,1:T(8,128)} reshape(f32[7,2,4,64,16,64]{3,2,5,4,0,1:T(4,128)} %bitcast.271) | data formatting | bytes 29360128 | tf_op jit(solution)/shard_map/all_to_all | solution.py:85
  449.4 13.3 fusion.219
  462.7 11.1 fusion.112
  473.8 10.0 fusion.110
  483.8 10.4 fusion.108
  494.2 10.2 fusion.114
  504.4 10.4 subtract_bitcast_fusion
  523.2 13.1 pad_maximum_fusion.2
  536.3 27.2 %copy.52 = f32[7,2,256,16,64]{4,3,0,1,2:T(8,128)} copy(f32[7,2,256,16,64]{2,4,3,0,1:T(8,128)} %pad_maximum_fusion.2) | data formatting | bytes 29360128 | tf_op jit(solution)/shard_map/stack | solution.py:89
  563.5 23.1 %reshape.249 = f32[8,1,458752]{2,1,0:T(1,128)} reshape(f32[256,2,7,16,64]{4,3,2,1,0:T(8,128)} %bitcast.274) | data formatting | bytes 29360128
  592.1 318.7 %all-to-all-done.1 = f32[8,1,458752]{2,1,0:T(1,128)} async-done(((f32[8,1,458752]{2,1,0:T(1,128)}), f32[8,1,458752]{2,1,0:T(1,128)}, u32[]{:S(2)}, u32[]{:S(2)}) %all-to-all-start.1) | async-done | bytes 14680096 | tf_op jit(solution)/shard_map/all_to_all | solution.py:90
  910.8 42.5 %reduce.3 = f32[8,458752]{1,0:T(8,128)} reduce(f32[8,1,458752]{2,1,0:T(1,128)} %all-to-all-done.1, f32[]{:T(128)} %broadcast.529), dimensions={1}, to_apply=%all_to_all.46.reduce_sub_computation | reduce | bytes 29360132 | tf_op jit(solution)/shard_map/all_to_all | solution.py:90
  953.3 26.2 %reshape.250 = f32[256,2,7,16,64]{4,3,2,1,0:T(8,128)} reshape(f32[8,458752]{1,0:T(8,128)} %reduce.3) | data formatting | bytes 29360128
  979.5 22.4 %copy.54 = f32[7,2,32,8,16,64]{5,4,3,2,1,0:T(8,128)} copy(f32[7,2,32,8,16,64]{5,4,0,1,2,3:T(8,128)} %bitcast.272) | data formatting | bytes 29360128 | tf_op jit(solution)/shard_map/all_to_all | solution.py:90
  1001.9 30.6 %fusion = f32[7,32,64,256]{3,2,1,0:T(8,128)} fusion(f32[7,2,32,128,64]{4,3,2,1,0:T(8,128)} %bitcast.268, f32[128]{0:T(128)S(1)} %fusion.134), kind=kOutput, calls=%fused_computation.17 | convolution fusion | flops 5637636096 | bytes 29360640 | tf_op jit(solution)/shard_map/fzky,kn->fzyn/dot_general | solution.py:91
  1032.6 32.5 %fusion.17 = f32[7,32,64,256]{3,2,1,0:T(8,128)} fusion(f32[7,32,64,256]{3,2,1,0:T(8,128)} %fusion, f32[7,2,32,128,64]{4,3,2,1,0:T(8,128)} %bitcast.269, f32[128]{0:T(128)S(1)} %fusion.134), kind=kOutput, calls=%fused_computation.41 | convolution fusion | flops 5641306112 | bytes 44040704 | tf_op jit(solution)/shard_map/fzky,kn->fzyn/dot_general | solution.py:91
  1077.3 11.2 negate_bitcast_fusion
  1088.4 12.8 convolution_bitcast_fusion
  1101.2 55.2 %fusion.16 = (f32[1,6,2,32,16,64]{4,5,3,1,2,0:T(8,128)}, f32[1,6,2,32,16,64]{4,5,3,1,2,0:T(8,128)}, f32[1,6,2,32,16,64]{4,5,3,1,2,0:T(8,128)}, f32[1,6,2,32,16,6...) fusion(f32[6,1,32,128,64]{3,4,2,0,1:T(8,128)S(1)} %negate_bitca, ...), kind=kLoop, calls=%fused_computation.38 | loop fusion | flops 3145728 | bytes 25165824 | tf_op jit(solution)/shard_map/stack | solution.py:115
  1244.5 20.5 reshape.251
  1265.0 280.5 %all_to_all.60 = f32[8,1,393216]{2,1,0:T(1,128)} all-to-all(f32[8,1,393216]{2,1,0:T(1,128)} %reshape.251), channel_id=1, replica_groups=mesh['grp'=4,'slab'=8] {'slab'}, dimensions={0} | all-to-all | bytes 25165824 | tf_op jit(solution)/shard_map/all_to_all | solution.py:114
  1545.4 37.0 %reduce.4 = f32[8,393216]{1,0:T(8,128)} reduce(f32[8,1,393216]{2,1,0:T(1,128)} %all_to_all.60, f32[]{:T(128)} %broadcast.529), dimensions={1}, to_apply=%all_to_all.50.reduce_sub_computation | reduce | bytes 25165828 | tf_op jit(solution)/shard_map/all_to_all | solution.py:114
  1582.5 22.6 %reshape.252 = f32[8,6,2,32,16,64]{5,4,3,2,1,0:T(8,128)} reshape(f32[8,393216]{1,0:T(8,128)} %reduce.4) | data formatting | bytes 25165824
  1605.1 17.1 copy.65
  1622.2 18.0 fusion.218
  1640.3 11.0 copy.79
  1651.2 11.4 fusion.122
  1671.5 10.8 copy.80
  1682.3 10.3 fusion.118
  1712.6 11.4 pad_maximum_fusion.4
  1724.0 23.8 %copy.68 = f32[6,2,256,16,64]{4,3,0,1,2:T(8,128)} copy(f32[6,2,256,16,64]{2,4,3,0,1:T(8,128)} %pad_maximum_fusion.4) | data formatting | bytes 25165824 | tf_op jit(solution)/shard_map/stack | solution.py:122
  1747.8 33.3 %reshape.253 = f32[4,1,786432]{2,1,0:T(1,128)} reshape(f32[256,2,6,16,64]{4,3,2,1,0:T(8,128)} %bitcast.277) | data formatting | bytes 25165824
  1796.4 14.5 psum.7
  1817.7 107.0 %all-to-all-done.3 = f32[4,1,786432]{2,1,0:T(1,128)} async-done(((f32[4,1,786432]{2,1,0:T(1,128)}), f32[4,1,786432]{2,1,0:T(1,128)}, u32[]{:S(2)}, u32[]{:S(2)}) %all-to-all-start.3) | async-done | bytes 12582944 | tf_op jit(solution)/shard_map/all_to_all | solution.py:123
  1924.6 39.8 %reduce.5 = f32[4,786432]{1,0:T(4,128)} reduce(f32[4,1,786432]{2,1,0:T(1,128)} %all-to-all-done.3, f32[]{:T(128)} %broadcast.529), dimensions={1}, to_apply=%all_to_all.51.reduce_sub_computation | reduce | bytes 25165828 | tf_op jit(solution)/shard_map/all_to_all | solution.py:123
  1964.4 31.9 %reshape.254 = f32[256,2,6,16,64]{4,3,2,1,0:T(8,128)} reshape(f32[4,786432]{1,0:T(4,128)} %reduce.5) | data formatting | bytes 25165824
  1996.4 30.3 %copy.86 = f32[6,2,4,64,16,64]{5,2,4,3,0,1:T(4,128)} copy(f32[6,2,4,64,16,64]{5,4,0,1,3,2:T(8,128)} %bitcast.278) | data formatting | bytes 25165824 | tf_op jit(solution)/shard_map/all_to_all | solution.py:123
  2026.6 23.2 %all_to_all.54 = f32[6,2,64,16,256]{4,3,2,0,1:T(8,128)} reshape(f32[6,2,64,16,4,64]{5,4,3,2,0,1:T(4,128)} %bitcast.279) | data formatting | bytes 25165824 | tf_op jit(solution)/shard_map/all_to_all | solution.py:123
  2049.8 9.9 fusion.22
  (168 shorter events, 257.3 us)
Async XLA Ops:
  0.0 9.1 copy-start.23
  0.5 8.6 copy-start.28
  4.4 489.8 %copy-start.21 = (s32[256]{0:T(256)}, s32[256]{0:T(256)S(1)}, u32[]{:S(2)}) copy-start(s32[256]{0:T(256)S(1)} %get-tuple-element.6) | copy-start | bytes 3076
  5.0 4.2 copy-start.25
  9.7 2.2 slice-start
  10.1 3.2 slice-start.1
  462.7 11.1 copy-start.2
  462.7 21.1 slice-start.7
  473.7 10.1 slice-start.8
  586.5 324.2 %all-to-all-start.1 = ((f32[8,1,458752]{2,1,0:T(1,128)}), f32[8,1,458752]{2,1,0:T(1,128)}, u32[]{:S(2)}, u32[]{:S(2)}) async-start(f32[8,1,458752]{2,1,0:T(1,128)} %reshape.249), calls=%async_computation.1 | async-start | bytes 29360128 | tf_op jit(solution)/shard_map/all_to_all | solution.py:90
  1065.1 10.1 copy-start
  1226.0 3.9 copy-start.12
  1226.0 6.0 copy-start.11
  1229.9 4.2 copy-start.10
  1232.0 4.2 copy-start.9
  1234.1 4.1 copy-start.7
  1236.2 4.1 copy-start.8
  1640.3 11.0 copy-start.22
  1651.2 11.4 copy-start.4
  1682.3 10.3 copy-start.3
  1692.7 8.9 copy-start.6
  1701.6 6.9 copy-start.5
  1781.1 143.5 %all-to-all-start.3 = ((f32[4,1,786432]{2,1,0:T(1,128)}), f32[4,1,786432]{2,1,0:T(1,128)}, u32[]{:S(2)}, u32[]{:S(2)}) async-start(f32[4,1,786432]{2,1,0:T(1,128)} %reshape.253), calls=%async_computation.3 | async-start | bytes 25165824 | tf_op jit(solution)/shard_map/all_to_all | solution.py:123
  1790.2 20.7 copy-start.27
  1790.2 23.3 %copy-start.30 = (f32[8]{0:T(128)S(1)}, f32[8]{0:T(128)}, u32[]{:S(2)}) copy-start(f32[8]{0:T(128)} %param.9) | copy-start | bytes 100
  1790.2 23.3 %copy-start.31 = (f32[8]{0:T(128)S(1)}, f32[8]{0:T(128)}, u32[]{:S(2)}) copy-start(f32[8]{0:T(128)} %param.8) | copy-start | bytes 100
  1790.2 23.8 %copy-start.33 = (s32[64]{0:T(128)S(1)}, s32[64]{0:T(128)}, u32[]{:S(2)}) copy-start(s32[64]{0:T(128)} %get-tuple-element.12) | copy-start | bytes 772
  1790.2 23.9 %copy-start.32 = (f32[16]{0:T(128)S(1)}, f32[16]{0:T(128)}, u32[]{:S(2)}) copy-start(f32[16]{0:T(128)} %get-tuple-element.48) | copy-start | bytes 196
  2049.8 9.9 copy-start.1
  2082.0 8.9 copy-start.24
  2082.1 8.9 copy-start.26
  2082.1 8.9 copy-start.29
  2090.9 3.9 copy-start.13
  2091.0 3.9 copy-start.14
  2091.0 3.9 copy-start.15
  2091.0 4.0 copy-start.16
  2091.0 13.3 slice-start.2
  2094.6 9.8 slice-start.4
  2094.8 9.5 copy-start.17
  2094.8 9.5 copy-start.18
  2095.0 10.2 slice-start.3
  2095.0 11.4 slice-start.5
  2095.0 12.6 slice-start.6
  2115.3 3.5 copy-start.19
  2115.3 4.1 copy-start.20
